TPU v7x, 32 devices: a whole 2x2x4 slice. The times are simulated.
32 devices in a mesh: row: 2 (over y), col: 8 (over z, x), layer: 2 (over core).
Axes of the slice: x: 2, y: 2, z: 4, core: 2. Of those that a mesh axis runs over, the one named last changes fastest.
Arguments:
- anomaly_x: bfloat16 [8, 4096, 4096], P(None, 'row', ('layer', 'col')), may hold values from -0.09375 to 0.09375
- anomaly_y: bfloat16 [8, 4096, 4096], P(None, 'col', ('layer', 'row')), may hold values from -6 to 6
Outputs:
- covariance: bfloat16 [8, 4096, 4096], P('layer', 'row', 'col')
All inputs are finite; a program needn't handle non-finite values.
Results may differ from a plain program's by a relative error of at most 0.001.
Values may be sent and summed in bfloat16 or wider, within the bound.
A program may use at most 192 MiB of HBM per device.

v0:
```python
import functools

import jax
import jax.numpy as jnp
from jax import lax
from jax.experimental import pallas as pl
from jax.experimental.pallas import tpu as pltpu
from jax.sharding import PartitionSpec as P

LANES = 128
HALVES = 2
MESH = pl.DeviceIdType.MESH
NT = (((1,), (1,)), ((), ()))


def gathered(anomaly_x, anomaly_y):
    panel_x = lax.all_gather(anomaly_x, "col", axis=2, tiled=True)
    partial_tile = jnp.einsum(
        "bik,bjk->bij",
        panel_x,
        lax.all_gather(anomaly_y, "row", axis=2, tiled=True),
        preferred_element_type=jnp.float32,
    )
    summed = lax.psum_scatter(partial_tile, "layer", scatter_dimension=0, tiled=True)
    return summed.astype(jnp.bfloat16)


def kernel(
    sizes, x_ref, y_ref, o_ref, xg, yg, og, local_sem,
    x_send, x_recv, xf_send, xf_recv, y_send, y_recv, yf_send, yf_recv, o_send, o_recv,
):
    rows, planes, lines, layers = sizes
    y, col, c = lax.axis_index("row"), lax.axis_index("col"), lax.axis_index("layer")
    z, x = col // lines, lax.rem(col, lines)
    depth_x, depth_y = x_ref.shape[2], y_ref.shape[2]
    height = x_ref.shape[1]
    group = depth_x * planes * lines
    steps = HALVES
    span = planes // HALVES
    q = lax.rem(z, span)
    base = z - q

    def plane(d):
        return lax.rem(z + d + planes, planes)

    def near(d):
        return lax.rem(q + d + span, span)

    def core(e):
        return lax.rem(c + e + layers, layers)

    def dev(yy, zz, xx, cc):
        return {"row": yy, "col": zz * lines + xx, "layer": cc}

    def xcols(cc, zz, xx):
        return pl.ds(pl.multiple_of(cc * group + (zz * lines + xx) * depth_x, depth_x), depth_x)

    def ycols(cc, yy):
        return pl.ds(pl.multiple_of(cc * group + yy * depth_y, depth_y), depth_y)

    def batch(qq, cc, s):
        return cc * planes + qq * steps + s

    xline = [lax.rem(x + d, lines) for d in range(1, lines)]
    yline = [lax.rem(y + d, rows) for d in range(1, rows)]
    peers = [dev(y, plane(d), x, core(e)) for d in range(planes) for e in range(layers) if d or e]
    peers += [dev(y, z, xx, c) for xx in xline] + [dev(yy, z, x, c) for yy in yline]
    barrier = pltpu.get_barrier_semaphore()
    for peer in peers:
        pl.semaphore_signal(barrier, inc=1, device_id=peer, device_id_type=MESH)
    pl.semaphore_wait(barrier, len(peers))

    sent = []

    def push(src, dst, s, r, to):
        cp = pltpu.make_async_remote_copy(
            src_ref=src, dst_ref=dst, send_sem=s, recv_sem=r, device_id=to, device_id_type=MESH
        )
        cp.start()
        sent.append(cp)

    def landed(dst, s, r):
        pltpu.make_async_remote_copy(
            src_ref=dst, dst_ref=dst, send_sem=s, recv_sem=r, device_id=peers[0], device_id_type=MESH
        ).wait_recv()

    def send_x(s, d, e):
        i = (s * planes + d) * layers + e
        to = plane(d)
        push(x_ref.at[batch(lax.rem(to, span), core(e), s)], xg.at[s, :, xcols(c, z, x)],
             x_send.at[i], x_recv.at[i], dev(y, to, x, core(e)))

    def send_y(s, d, e):
        i = (s * span + d) * layers + e
        push(y_ref.at[batch(near(d), core(e), s)], yg.at[s, d, :, ycols(c, y)],
             y_send.at[i], y_recv.at[i], dev(y, base + near(d), x, core(e)))

    def forward_x(s, d, e, src=None):
        i = (s * planes + d) * layers + e
        zone = xg.at[s, :, xcols(core(-e), plane(-d), x)]
        if src is None:
            landed(zone, x_send.at[i], x_recv.at[i])
        for j, xx in enumerate(xline):
            k = i * len(xline) + j
            push(zone if src is None else src, zone, xf_send.at[k], xf_recv.at[k], dev(y, z, xx, c))

    def forward_y(s, d, e, src=None):
        i = (s * span + d) * layers + e
        zone = yg.at[s, d, :, ycols(core(-e), y)]
        if src is None:
            landed(zone, y_send.at[i], y_recv.at[i])
        for j, yy in enumerate(yline):
            k = i * len(yline) + j
            push(zone if src is None else src, zone, yf_send.at[k], yf_recv.at[k], dev(yy, z, x, c))

    far = planes // 2
    order = [(far, e) for e in range(layers)]
    order += [(d, e) for d in range(1, planes) if d != far for e in range(layers)]
    keeps = []
    for s in range(steps):
        own = batch(q, c, s)
        forward_x(s, 0, 0, x_ref.at[own])
        forward_y(s, 0, 0, y_ref.at[own])
        keep_x = pltpu.make_async_copy(x_ref.at[own], xg.at[s, :, xcols(c, z, x)], local_sem.at[2 * s])
        keep_y = pltpu.make_async_copy(y_ref.at[own], yg.at[s, 0, :, ycols(c, y)], local_sem.at[2 * s + 1])
        keep_x.start()
        keep_y.start()
        keeps.append((keep_x, keep_y))
        for e in range(1, layers):
            send_x(s, 0, e)
            send_y(s, 0, e)
        for d, e in order:
            send_x(s, d, e)
            if d < span:
                send_y(s, d, e)

    tile = min(height, 256)

    def multiply(s, d):
        def body(r, _):
            at = pl.ds(pl.multiple_of(r * tile, tile), tile)
            og[s, d, at, :] = lax.dot_general(
                xg[s, at, :], yg[s, d], NT, preferred_element_type=jnp.float32
            ).astype(jnp.bfloat16)
            return 0

        lax.fori_loop(0, height // tile, body, 0)

    outs = []
    for s in range(steps):
        for e in range(1, layers):
            forward_x(s, 0, e)
            forward_y(s, 0, e)
        for d in list(range(1, far)) + list(range(far + 1, planes)) + [far]:
            for e in range(layers):
                forward_x(s, d, e)
                if d < span:
                    forward_y(s, d, e)
        for keep in keeps[s]:
            keep.wait()
        for d in range(planes):
            for e in range(layers):
                for j in range(len(xline)):
                    xx = lax.rem(x - (j + 1) + lines, lines)
                    k = ((s * planes + d) * layers + e) * len(xline) + j
                    landed(xg.at[s, :, xcols(core(-e), plane(-d), xx)], xf_send.at[k], xf_recv.at[k])
        for d in range(span):
            for e in range(layers):
                for j in range(len(yline)):
                    yy = lax.rem(y - (j + 1) + rows, rows)
                    k = ((s * span + d) * layers + e) * len(yline) + j
                    landed(yg.at[s, d, :, ycols(core(-e), yy)], yf_send.at[k], yf_recv.at[k])
        for d in list(range(1, span)):
            multiply(s, d)
            push(og.at[s, d], o_ref.at[q * steps + s], o_send.at[s * span + d], o_recv.at[s * span + d],
                 dev(y, base + near(-d), x, c))
        multiply(s, 0)
        keep = pltpu.make_async_copy(og.at[s, 0], o_ref.at[q * steps + s], local_sem.at[2 * steps + s])
        keep.start()
        outs.append(keep)
    for s in range(steps):
        for d in range(1, span):
            landed(o_ref.at[near(d) * steps + s], o_send.at[s * span + d], o_recv.at[s * span + d])
        outs[s].wait()
    for cp in sent:
        cp.wait_send()


def routed(sizes, anomaly_x, anomaly_y):
    rows, planes, lines, layers = sizes
    _, height, depth_x = anomaly_x.shape
    width, depth_y = anomaly_y.shape[1:]
    members = depth_y * rows * layers
    span, steps = planes // HALVES, HALVES
    bx, by = steps * planes * layers, steps * span * layers
    dma = pltpu.SemaphoreType.DMA
    any_ = pl.BlockSpec(memory_space=pl.ANY)
    fx, fy = max(1, bx * (lines - 1)), max(1, by * (rows - 1))
    kind = anomaly_x.dtype
    return pl.pallas_call(
        functools.partial(kernel, sizes),
        out_shape=jax.ShapeDtypeStruct((planes, height, width), jnp.bfloat16),
        in_specs=[any_, any_],
        out_specs=any_,
        scratch_shapes=[
            pltpu.VMEM((steps, height, members), kind),
            pltpu.VMEM((steps, span, width, members), kind),
            pltpu.VMEM((steps, span, height, width), jnp.bfloat16),
            dma((3 * steps,)),
            dma((bx,)), dma((bx,)), dma((fx,)), dma((fx,)),
            dma((by,)), dma((by,)), dma((fy,)), dma((fy,)),
            dma((steps * span,)), dma((steps * span,)),
        ],
        compiler_params=pltpu.CompilerParams(
            collective_id=0, has_side_effects=True, vmem_limit_bytes=63 * 2**20
        ),
    )(anomaly_x, anomaly_y)


def on_device(mesh, anomaly_x, anomaly_y):
    rows, cols, layers = (mesh.shape[name] for name in ("row", "col", "layer"))
    batches, _, depth_x = anomaly_x.shape
    planes = batches // layers
    if batches % layers or planes % HALVES or cols % planes or depth_x % LANES:
        return gathered(anomaly_x, anomaly_y)
    return routed((rows, planes, cols // planes, layers), anomaly_x, anomaly_y)


def solution(mesh):
    placed = (P(None, "row", ("layer", "col")), P(None, "col", ("layer", "row")))
    return jax.shard_map(
        functools.partial(on_device, mesh),
        mesh=mesh, in_specs=placed, out_specs=P("layer", "row", "col"), check_vma=False,
    )
```

profile of v0, /device:TPU:0, one launch (start us, length us, event | category | flops | bytes accessed | tf_op | source)
XLA Modules:
  0.0 501.5 jit_solution(15394165146036573926)
XLA Ops:
  0.0 494.2 %shard_map.28 = bf16[4,2048,512]{2,1,0:T(8,128)(2,1)} custom-call(bf16[8,2048,256]{2,1,0:T(8,128)(2,1)} %x_ref.1, bf16[8,512,1024]{2,1,0:T(8,128)(2,1)} %y_ref.1), custom_call_target="tpu_custom_call" | custom-call | tf_op jit(solution)/shard_map/pallas_call | solution.py:200
  494.2 7.3 %copy.4 = bf16[4,2048,512]{2,1,0:T(8,128)(2,1)} copy(bf16[4,2048,512]{2,1,0:T(8,128)(2,1)} %shard_map.28) | data formatting | bytes 16777216
where the time goes:
time: 502 us
  Pallas kernels  494 us (98%)
  local copies, waits for them, and re-layouts  7.32 us (1%)
    pallas_call x1, Pallas kernels, routed(): pl.pallas_call(functools.partial(kernel, sizes), out_shape=jax.ShapeDtype...  494 us

commit v1 on v0

v1 whole, which is shorter than its diff:
```python
import functools

import jax
import jax.numpy as jnp
from jax import lax
from jax.experimental import pallas as pl
from jax.experimental.pallas import tpu as pltpu
from jax.sharding import PartitionSpec as P

LANES = 128
MESH = pl.DeviceIdType.MESH
NT = (((1,), (1,)), ((), ()))


def gathered(anomaly_x, anomaly_y):
    panel_x = lax.all_gather(anomaly_x, "col", axis=2, tiled=True)
    partial_tile = jnp.einsum(
        "bik,bjk->bij",
        panel_x,
        lax.all_gather(anomaly_y, "row", axis=2, tiled=True),
        preferred_element_type=jnp.float32,
    )
    summed = lax.psum_scatter(partial_tile, "layer", scatter_dimension=0, tiled=True)
    return summed.astype(jnp.bfloat16)


def plan():
    recv = {}

    def add(*key):
        recv[key] = len(recv)

    for rel in range(4):
        for ec in range(2):
            for ex in range(2):
                if rel or ec or ex:
                    add("x0", rel, ec, ex)
    for ec in range(2):
        for ex in range(2):
            if ec or ex:
                add("x1", ec, ex)
            for yr in range(2):
                if ec or ex or yr:
                    add("y0", ec, ex, yr)
                    add("y1", 0, ec, ex, yr)
                add("y1", 1, ec, ex, yr)
    for kind in ("out0", "out1", "out2"):
        add(kind)
    return recv


RECV = plan()
SENDS = 48


def kernel(
    sizes, x_ref, y_ref, o_ref, xg, yg0, yg1, og0, og1,
    local_sem, send_sem, recv_sem, up_send, up_recv, near_send, far_send, near_recv, far_recv,
    o0_send, o0_keep, o1_send, o1_keep,
):
    rows, planes, lines, layers = sizes
    y, col, c = lax.axis_index("row"), lax.axis_index("col"), lax.axis_index("layer")
    z, x = col // lines, lax.rem(col, lines)
    depth_x, depth_y = x_ref.shape[2], y_ref.shape[2]
    height, width = x_ref.shape[1], y_ref.shape[1]
    group = depth_x * planes * lines
    pair = depth_x * lines
    chunk = og0.shape[1]
    count = height // chunk
    slots0, slots1 = og0.shape[0], og1.shape[0]

    half = z // 2
    mid, end = 1 + half, 3 * half
    inner = (z == 1) | (z == 2)
    partner = z + 1 - 2 * lax.rem(z, 2)
    across = planes - 1 - z
    level = [z, partner, planes - 1 - mid, planes - 1 - end]

    def core(e):
        return lax.rem(c + e, layers)

    def line(e):
        return lax.rem(x + e, lines)

    def row(e):
        return lax.rem(y + e, rows)

    def dev(yy, zz, xx, cc):
        return {"row": yy, "col": zz * lines + xx, "layer": cc}

    def batch(ec, ex, s):
        return core(ec) * planes + line(ex) * 2 + s

    def xcols(rel, ec, ex):
        return pl.ds(pl.multiple_of(core(ec) * group + (level[rel] * lines + line(ex)) * depth_x, depth_x), depth_x)

    def xpair(rel, ec):
        return pl.ds(pl.multiple_of(core(ec) * group + level[rel] * pair, pair), pair)

    def ycols(ec, er):
        return pl.ds(pl.multiple_of(core(ec) * group + row(er) * depth_y, depth_y), depth_y)

    def y0zone(ec, ex, er):
        return yg0.at[pl.ds(pl.multiple_of(line(ex) * width, width), width), ycols(ec, er)]

    def y1zone(rel, ec, ex, er):
        at = lax.rem(level[rel], 2) * lines * width + line(ex) * width
        return yg1.at[pl.ds(pl.multiple_of(at, width), width), ycols(ec, er)]

    def rowsof(r):
        return pl.ds(pl.multiple_of(r * chunk, chunk), chunk)

    def tile(q):
        return pl.ds(pl.multiple_of(q * width, width), width)

    peers = [dev(y, z, line(ex), core(ec)) for ec in range(2) for ex in range(2) if ec or ex]
    peers += [dev(row(1), z, x, c), dev(y, partner, x, c), dev(y, partner, line(1), c), dev(y, across, x, c)]
    barrier = pltpu.get_barrier_semaphore()
    for peer in peers:
        pl.semaphore_signal(barrier, inc=1, device_id=peer, device_id_type=MESH)
    pl.semaphore_wait(barrier, len(peers))

    over_y, over_half, over_mid = dev(row(1), z, x, c), dev(y, partner, x, c), dev(y, across, x, c)

    def remote(src, dst, s, r, to):
        return pltpu.make_async_remote_copy(
            src_ref=src, dst_ref=dst, send_sem=s, recv_sem=r, device_id=to, device_id_type=MESH
        )

    def landed(dst, sem):
        remote(dst, dst, sem, sem, over_y).wait_recv()

    sent = []

    def push(log, src, dst, key, to):
        cp = remote(src, dst, send_sem.at[len(log)], recv_sem.at[RECV[key]], to)
        cp.start()
        log.append(cp)

    def await_x0(rel, ec, ex):
        landed(xg.at[0, :, xcols(rel, ec, ex)], recv_sem.at[RECV["x0", rel, ec, ex]])

    def await_x1(ec, ex):
        landed(xg.at[1, :, xcols(0, ec, ex)], recv_sem.at[RECV["x1", ec, ex]])

    def await_y0(ec, ex, er):
        landed(y0zone(ec, ex, er), recv_sem.at[RECV["y0", ec, ex, er]])

    def await_y1(rel, ec, ex, er):
        landed(y1zone(rel, ec, ex, er), recv_sem.at[RECV["y1", rel, ec, ex, er]])

    def send_x0(log, rel, ec, ex, to, there):
        zone = xg.at[0, :, xcols(rel, ec, ex)]
        src = zone if rel or ec or ex else x_ref.at[batch(0, 0, 0)]
        push(log, src, zone, ("x0", there, ec, ex), to)

    def send_y0(log, ec, ex):
        zone = y0zone(ec, ex, 0)
        src = zone if ec or ex else y_ref.at[batch(0, 0, 0)]
        push(log, src, zone, ("y0", ec, ex, 1), over_y)

    def send_y1(log, rel, ec, ex, to, there, er):
        zone = y1zone(rel, ec, ex, 0)
        src = zone if rel or ec or ex else y_ref.at[batch(0, 0, 1)]
        push(log, src, zone, ("y1", there, ec, ex, er), to)

    def spread(ec, ex):
        to = dev(y, z, line(ex), core(ec))
        own = (0, 0)
        push(sent, x_ref.at[batch(ec, ex, 0)], xg.at[0, :, xcols(0, *own)], ("x0", 0, ec, ex), to)
        push(sent, y_ref.at[batch(ec, ex, 1)], y1zone(0, *own, 0), ("y1", 0, ec, ex, 0), to)
        push(sent, x_ref.at[batch(ec, ex, 1)], xg.at[1, :, xcols(0, *own)], ("x1", ec, ex), to)
        push(sent, y_ref.at[batch(ec, ex, 0)], y0zone(*own, 0), ("y0", ec, ex, 0), to)

    def spread_line():
        own = (0, 0)
        for what in range(4):
            for ec in range(2):
                to = dev(y, z, line(1), core(ec))
                if what == 0:
                    push(sent, x_ref.at[batch(ec, 1, 0)], xg.at[0, :, xcols(0, *own)], ("x0", 0, ec, 1), to)
                elif what == 1:
                    push(sent, y_ref.at[batch(ec, 1, 1)], y1zone(0, *own, 0), ("y1", 0, ec, 1, 0), to)
                elif what == 2:
                    push(sent, x_ref.at[batch(ec, 1, 1)], xg.at[1, :, xcols(0, *own)], ("x1", ec, 1), to)
                else:
                    push(sent, y_ref.at[batch(ec, 1, 0)], y0zone(*own, 0), ("y0", ec, 1, 0), to)

    send_x0(sent, 0, 0, 0, over_half, 1)
    spread(1, 0)
    spread_line()
    keeps = [
        pltpu.make_async_copy(x_ref.at[batch(0, 0, s)], xg.at[s, :, xcols(0, 0, 0)], local_sem.at[s]) for s in range(2)
    ] + [
        pltpu.make_async_copy(y_ref.at[batch(0, 0, 0)], y0zone(0, 0, 0), local_sem.at[2]),
        pltpu.make_async_copy(y_ref.at[batch(0, 0, 1)], y1zone(0, 0, 0, 0), local_sem.at[3]),
    ]
    for keep in keeps:
        keep.start()

    def out0(k, e):
        slot = lax.rem(k, slots0)
        src = og0.at[slot, :, tile(line(e))]
        dst = o_ref.at[x * 2, rowsof(k)]
        if e == 0:
            return pltpu.make_async_copy(src, dst, o0_keep.at[slot])
        return remote(src, dst, o0_send.at[slot], recv_sem.at[RECV[("out0",)]], dev(y, z, line(1), c))

    def free0(k):
        out0(k, 0).wait()
        out0(k, 1).wait_send()

    def product0(k):
        pl.when(k >= slots0)(lambda: free0(k - slots0))
        og0[lax.rem(k, slots0)] = lax.dot_general(
            xg[0, rowsof(k), :], yg0[...], NT, preferred_element_type=jnp.float32
        ).astype(jnp.bfloat16)
        out0(k, 0).start()
        out0(k, 1).start()

    def out1(r, ez, ex):
        slot = lax.rem(r, slots1)
        zz = lax.rem(level[ez], 2)
        src = og1.at[slot, :, tile(zz * lines + line(ex))]
        dst = o_ref.at[x * 2 + 1, rowsof(r)]
        if not ez and not ex:
            return pltpu.make_async_copy(src, dst, o1_keep.at[slot])
        kind = "out1" if ez == 0 or ex == 0 else "out2"
        return remote(src, dst, o1_send.at[slot * 3 + ez * 2 + ex - 1], recv_sem.at[RECV[(kind,)]],
                      dev(y, level[ez], line(ex), c))

    def free1(r):
        out1(r, 0, 0).wait()
        for ez, ex in ((1, 1), (1, 0), (0, 1)):
            out1(r, ez, ex).wait_send()

    def near(r, ec, to, sems):
        zone = xg.at[1, rowsof(r), xpair(0, ec)]
        return remote(zone, zone, near_send.at[r * 2 + ec], sems.at[r * 2 + ec], to)

    def far(r, ec):
        zone = xg.at[1, rowsof(r), xpair(1, ec)]
        return remote(zone, zone, far_send.at[r * 2 + ec], far_recv.at[r * 2 + ec], over_mid)

    def send_near(r):
        for ec in range(2):
            near(r, ec, over_mid, near_recv).start()

    def send_far(r):
        for ec in range(2):
            landed(xg.at[1, rowsof(r), xpair(1, ec)], up_recv.at[r * 2 + ec])
            far(r, ec).start()

    def product1(r):
        for ec in range(2):
            landed(xg.at[1, rowsof(r), xpair(2, ec)], near_recv.at[r * 2 + ec])
            landed(xg.at[1, rowsof(r), xpair(3, ec)], far_recv.at[r * 2 + ec])
        pl.when(r >= slots1)(lambda: free1(r - slots1))
        slot, wide = lax.rem(r, slots1), lines * width

        def part(q, _):
            at = pl.ds(pl.multiple_of(q * wide, wide), wide)
            og1[slot, :, at] = lax.dot_general(
                xg[1, rowsof(r), :], yg1[at, :], NT, preferred_element_type=jnp.float32
            ).astype(jnp.bfloat16)
            return 0

        lax.fori_loop(0, 2, part, 0)
        for ez, ex in ((1, 1), (1, 0), (0, 1), (0, 0)):
            out1(r, ez, ex).start()

    ahead = 4

    @pl.when(inner)
    def _():
        log = list(sent)
        send_x0(log, 0, 0, 0, over_mid, 2)
        send_y1(log, 0, 0, 0, over_y, 0, 1)

        def own(ec, ex):
            await_x0(0, ec, ex)
            send_x0(log, 0, ec, ex, over_mid, 2)
            send_x0(log, 0, ec, ex, over_half, 1)

        def outer(ec, ex):
            await_x0(1, ec, ex)
            send_x0(log, 1, ec, ex, over_mid, 3)

        def other(rel, ec, ex):
            await_x0(rel, ec, ex)
            send_x0(log, rel, ec, ex, over_half, rel)

        def side0(ec, ex):
            await_y0(ec, ex, 0)
            send_y0(log, ec, ex)

        def side1(rel, ec, ex):
            await_y1(rel, ec, ex, 0)
            send_y1(log, rel, ec, ex, over_y, rel, 1)

        own(1, 0)
        side1(0, 1, 0)
        send_y0(log, 0, 0)
        own(0, 1)
        outer(0, 0)
        other(2, 0, 0)
        own(1, 1)
        outer(1, 0)
        other(2, 1, 0)
        side1(0, 0, 1)
        other(2, 0, 1)
        side1(1, 0, 0)
        side1(0, 1, 1)
        side1(1, 1, 0)
        side0(1, 0)
        other(2, 1, 1)
        outer(0, 1)
        other(3, 0, 0)
        outer(1, 1)
        other(3, 1, 0)
        keeps[1].wait()
        await_x1(1, 0)
        await_x1(0, 1)
        await_x1(1, 1)
        send_near(0)
        send_near(1)
        side1(1, 0, 1)
        other(3, 0, 1)
        side0(0, 1)
        side1(1, 1, 1)
        other(3, 1, 1)
        side0(1, 1)
        for r in range(ahead):
            send_far(r)
            send_near(r + 2)
        keeps[0].wait()
        keeps[2].wait()
        keeps[3].wait()
        for rel in range(2):
            for ec in range(2):
                for ex in range(2):
                    await_y1(rel, ec, ex, 1)

        def both(r, _):
            product1(r)

            @pl.when(r + ahead < count)
            def _():
                send_far(r + ahead)

            @pl.when(r + ahead + 2 < count)
            def _():
                send_near(r + ahead + 2)

            @pl.when(r == 3)
            def _():
                for ec in range(2):
                    for ex in range(2):
                        await_y0(ec, ex, 1)

            @pl.when((r >= 3) & (r < 7))
            def _():
                def step(k, _):
                    product0((r - 3) * (count // 4) + k)
                    return 0

                lax.fori_loop(0, count // 4, step, 0)

            return 0

        lax.fori_loop(0, count, both, 0)
        for r in range(count):
            for ec in range(2):
                near(r, ec, over_mid, near_recv).wait_send()
                far(r, ec).wait_send()
        for r in range(count - slots1, count):
            free1(r)
        for k in range(count - slots0, count):
            free0(k)
        landed(o_ref.at[line(1) * 2], recv_sem.at[RECV[("out0",)]])
        landed(o_ref.at[line(1) * 2 + 1], recv_sem.at[RECV[("out1",)]])
        for cp in log:
            cp.wait_send()

    @pl.when(jnp.logical_not(inner))
    def _():
        log = list(sent)

        def own(ec, ex):
            await_x0(0, ec, ex)
            send_x0(log, 0, ec, ex, over_half, 1)

        def side0(ec, ex):
            await_y0(ec, ex, 0)
            send_y0(log, ec, ex)

        def down(ec, ex):
            if ec or ex:
                await_y1(0, ec, ex, 0)
            send_y1(log, 0, ec, ex, over_half, 1, 0)

        own(1, 0)
        down(0, 0)
        down(1, 0)
        send_y0(log, 0, 0)
        side0(1, 0)
        own(0, 1)
        own(1, 1)
        down(0, 1)
        down(1, 1)
        keeps[1].wait()
        await_x1(1, 0)
        await_x1(0, 1)
        await_x1(1, 1)
        for r in range(count):
            for ec in range(2):
                near(r, ec, over_half, up_recv).start()
        side0(0, 1)
        side0(1, 1)
        keeps[0].wait()
        keeps[2].wait()
        keeps[3].wait()
        for ec in range(2):
            for ex in range(2):
                await_y0(ec, ex, 1)
        for rel in range(1, 4):
            for ec in range(2):
                for ex in range(2):
                    await_x0(rel, ec, ex)

        def step(k, _):
            product0(k)
            return 0

        lax.fori_loop(0, count, step, 0)
        for r in range(count):
            for ec in range(2):
                near(r, ec, over_half, up_recv).wait_send()
        for k in range(count - slots0, count):
            free0(k)
        landed(o_ref.at[line(1) * 2], recv_sem.at[RECV[("out0",)]])
        landed(o_ref.at[x * 2 + 1], recv_sem.at[RECV[("out1",)]])
        landed(o_ref.at[line(1) * 2 + 1], recv_sem.at[RECV[("out2",)]])
        for cp in log:
            cp.wait_send()


def routed(sizes, anomaly_x, anomaly_y):
    rows, planes, lines, layers = sizes
    _, height, depth_x = anomaly_x.shape
    width, depth_y = anomaly_y.shape[1:]
    members = depth_y * rows * layers
    chunk, slots0, slots1 = height // 8, 4, 3
    count = height // chunk
    dma = pltpu.SemaphoreType.DMA
    any_ = pl.BlockSpec(memory_space=pl.ANY)
    kind = anomaly_x.dtype
    return pl.pallas_call(
        functools.partial(kernel, sizes),
        out_shape=jax.ShapeDtypeStruct((planes, height, width), jnp.bfloat16),
        in_specs=[any_, any_],
        out_specs=any_,
        scratch_shapes=[
            pltpu.VMEM((2, height, members), kind),
            pltpu.VMEM((lines * width, members), kind),
            pltpu.VMEM((2 * lines * width, members), kind),
            pltpu.VMEM((slots0, chunk, lines * width), jnp.bfloat16),
            pltpu.VMEM((slots1, chunk, 2 * lines * width), jnp.bfloat16),
            dma((4,)), dma((SENDS,)), dma((len(RECV),)),
            dma((2 * count,)), dma((2 * count,)), dma((2 * count,)), dma((2 * count,)), dma((2 * count,)), dma((2 * count,)),
            dma((slots0,)), dma((slots0,)), dma((3 * slots1,)), dma((slots1,)),
        ],
        compiler_params=pltpu.CompilerParams(
            collective_id=0, has_side_effects=True, vmem_limit_bytes=67043328
        ),
    )(anomaly_x, anomaly_y)


def on_device(mesh, anomaly_x, anomaly_y):
    rows, cols, layers = (mesh.shape[name] for name in ("row", "col", "layer"))
    batches, height, depth_x = anomaly_x.shape
    planes = batches // layers
    fits = rows == 2 and layers == 2 and batches == 8 and cols == 2 * planes
    if not fits or depth_x % LANES or height % 128:
        return gathered(anomaly_x, anomaly_y)
    return routed((rows, planes, cols // planes, layers), anomaly_x, anomaly_y)


def solution(mesh):
    placed = (P(None, "row", ("layer", "col")), P(None, "col", ("layer", "row")))
    return jax.shard_map(
        functools.partial(on_device, mesh),
        mesh=mesh, in_specs=placed, out_specs=P("layer", "row", "col"), check_vma=False,
    )
```

time: 502 us -> 393 us (0.78)
  Pallas kernels: 494 us -> 385 us
    pallas_call x1, Pallas kernels: 494 us -> 385 us  [routed(): pl.pallas_call(functools.partial(kernel, sizes), out_shape=jax.ShapeDtype...]
where the time goes in v1:
time: 393 us
  Pallas kernels  385 us (98%)
  local copies, waits for them, and re-layouts  7.32 us (2%)
    pallas_call x1, Pallas kernels, routed(): pl.pallas_call(functools.partial(kernel, sizes), out_shape=jax.ShapeDtype...  385 us

profile of v1, /device:TPU:0, one launch (start us, length us, event | category | flops | bytes accessed | tf_op | source)
XLA Modules:
  0.0 392.6 jit_solution(14480541204278655644)
XLA Ops:
  0.0 385.3 %shard_map.28 = bf16[4,2048,512]{2,1,0:T(8,128)(2,1)} custom-call(bf16[8,2048,256]{2,1,0:T(8,128)(2,1)} %x_ref.1, bf16[8,512,1024]{2,1,0:T(8,128)(2,1)} %y_ref.1), custom_call_target="tpu_custom_call" | custom-call | tf_op jit(solution)/shard_map/pallas_call | solution.py:458
  385.3 7.3 %copy.4 = bf16[4,2048,512]{2,1,0:T(8,128)(2,1)} copy(bf16[4,2048,512]{2,1,0:T(8,128)(2,1)} %shard_map.28) | data formatting | bytes 16777216

commit v2 on v1

--- a/solution.py
+++ b/solution.py
@@ -56,7 +56,7 @@
 def kernel(
     sizes, x_ref, y_ref, o_ref, xg, yg0, yg1, og0, og1,
     local_sem, send_sem, recv_sem, up_send, up_recv, near_send, far_send, near_recv, far_recv,
-    o0_send, o0_keep, o1_send, o1_keep,
+    o0_send, o0_keep, o1_send, o1_keep, acc,
 ):
     rows, planes, lines, layers = sizes
     y, col, c = lax.axis_index("row"), lax.axis_index("col"), lax.axis_index("layer")
@@ -68,6 +68,8 @@
     chunk = og0.shape[1]
     count = height // chunk
     slots0, slots1 = og0.shape[0], og1.shape[0]
+    last, wide = count - 1, lines * width
+    tails = [(0, chunk // 2), (chunk // 2, chunk // 4), (3 * chunk // 4, chunk // 4)]
 
     half = z // 2
     mid, end = 1 + half, 3 * half
@@ -246,17 +248,30 @@
         for ec in range(2):
             near(r, ec, over_mid, near_recv).start()
 
+    def far_tail(j, ec):
+        at, size = tails[j]
+        zone = xg.at[1, pl.ds(last * chunk + at, size), xpair(1, ec)]
+        k = (last + j) * 2 + ec
+        return remote(zone, zone, far_send.at[k], far_recv.at[k], over_mid)
+
     def send_far(r):
         for ec in range(2):
             landed(xg.at[1, rowsof(r), xpair(1, ec)], up_recv.at[r * 2 + ec])
             far(r, ec).start()
+
+    def send_tails():
+        for ec in range(2):
+            landed(xg.at[1, rowsof(last), xpair(1, ec)], up_recv.at[last * 2 + ec])
+        for j in range(len(tails)):
+            for ec in range(2):
+                far_tail(j, ec).start()
 
     def product1(r):
         for ec in range(2):
             landed(xg.at[1, rowsof(r), xpair(2, ec)], near_recv.at[r * 2 + ec])
             landed(xg.at[1, rowsof(r), xpair(3, ec)], far_recv.at[r * 2 + ec])
         pl.when(r >= slots1)(lambda: free1(r - slots1))
-        slot, wide = lax.rem(r, slots1), lines * width
+        slot = lax.rem(r, slots1)
 
         def part(q, _):
             at = pl.ds(pl.multiple_of(q * wide, wide), wide)
@@ -268,6 +283,56 @@
         lax.fori_loop(0, 2, part, 0)
         for ez, ex in ((1, 1), (1, 0), (0, 1), (0, 0)):
             out1(r, ez, ex).start()
+
+    def out_tail(j, ez, ex):
+        at, size = tails[j]
+        zz = lax.rem(level[ez], 2)
+        src = og1.at[last % slots1, pl.ds(at, size), tile(zz * lines + line(ex))]
+        dst = o_ref.at[x * 2 + 1, pl.ds(last * chunk + at, size)]
+        if not ez and not ex:
+            return pltpu.make_async_copy(src, dst, o1_keep.at[slots1 + j])
+        kind = "out1" if ez == 0 or ex == 0 else "out2"
+        return remote(src, dst, o1_send.at[(slots1 + j) * 3 + ez * 2 + ex - 1], recv_sem.at[RECV[(kind,)]],
+                      dev(y, level[ez], line(ex), c))
+
+    def members(ec, far_part):
+        third = planes - 1
+        if far_part:
+            return xpair(3, ec)
+        first = jnp.where(level[3] == 0, pair, 0)
+        return pl.ds(pl.multiple_of(core(ec) * group + first, pair), third * pair)
+
+    def terms(rows_at, cols_at, far_part):
+        total = None
+        for ec in range(2):
+            at = members(ec, far_part)
+            term = lax.dot_general(xg[1, rows_at, at], yg1[cols_at, at], NT, preferred_element_type=jnp.float32)
+            total = term if total is None else total + term
+        return total
+
+    def half_cols(q):
+        return pl.ds(pl.multiple_of(q * wide, wide), wide)
+
+    def product_last():
+        for ec in range(2):
+            landed(xg.at[1, rowsof(last), xpair(2, ec)], near_recv.at[last * 2 + ec])
+
+        def part(q, _):
+            acc[:, half_cols(q)] = terms(rowsof(last), half_cols(q), False)
+            return 0
+
+        lax.fori_loop(0, 2, part, 0)
+        free1(last - slots1)
+        for j, (at, size) in enumerate(tails):
+            for ec in range(2):
+                landed(xg.at[1, pl.ds(last * chunk + at, size), xpair(3, ec)], far_recv.at[(last + j) * 2 + ec])
+            for ez in (1, 0):
+                cols_at = half_cols(lax.rem(level[ez], 2))
+                og1[last % slots1, pl.ds(at, size), cols_at] = (
+                    acc[pl.ds(at, size), cols_at] + terms(pl.ds(last * chunk + at, size), cols_at, True)
+                ).astype(jnp.bfloat16)
+                for ex in (1, 0):
+                    out_tail(j, ez, ex).start()
 
     ahead = 4
 
@@ -344,13 +409,21 @@
         def both(r, _):
             product1(r)
 
-            @pl.when(r + ahead < count)
+            @pl.when(r + ahead < last)
             def _():
                 send_far(r + ahead)
 
-            @pl.when(r + ahead + 2 < count)
+            @pl.when(r == 0)
             def _():
-                send_near(r + ahead + 2)
+                send_near(last - 1)
+
+            @pl.when(r == 2)
+            def _():
+                send_near(last)
+
+            @pl.when(r + ahead == last)
+            def _():
+                send_tails()
 
             @pl.when(r == 3)
             def _():
@@ -368,12 +441,20 @@
 
             return 0
 
-        lax.fori_loop(0, count, both, 0)
+        lax.fori_loop(0, last, both, 0)
+        product_last()
         for r in range(count):
             for ec in range(2):
                 near(r, ec, over_mid, near_recv).wait_send()
-                far(r, ec).wait_send()
-        for r in range(count - slots1, count):
+                if r < last:
+                    far(r, ec).wait_send()
+        for j in range(len(tails)):
+            for ec in range(2):
+                far_tail(j, ec).wait_send()
+            for ez, ex in ((1, 1), (1, 0), (0, 1)):
+                out_tail(j, ez, ex).wait_send()
+            out_tail(j, 0, 0).wait()
+        for r in range(count - slots1, last):
             free1(r)
         for k in range(count - slots0, count):
             free0(k)
@@ -450,7 +531,7 @@
     _, height, depth_x = anomaly_x.shape
     width, depth_y = anomaly_y.shape[1:]
     members = depth_y * rows * layers
-    chunk, slots0, slots1 = height // 8, 4, 3
+    chunk, slots0, slots1 = height // 8, 2, 2
     count = height // chunk
     dma = pltpu.SemaphoreType.DMA
     any_ = pl.BlockSpec(memory_space=pl.ANY)
@@ -467,8 +548,9 @@
             pltpu.VMEM((slots0, chunk, lines * width), jnp.bfloat16),
             pltpu.VMEM((slots1, chunk, 2 * lines * width), jnp.bfloat16),
             dma((4,)), dma((SENDS,)), dma((len(RECV),)),
-            dma((2 * count,)), dma((2 * count,)), dma((2 * count,)), dma((2 * count,)), dma((2 * count,)), dma((2 * count,)),
-            dma((slots0,)), dma((slots0,)), dma((3 * slots1,)), dma((slots1,)),
+            dma((2 * count,)), dma((2 * count,)), dma((2 * count,)), dma((2 * count + 4,)), dma((2 * count,)), dma((2 * count + 4,)),
+            dma((slots0,)), dma((slots0,)), dma((3 * slots1 + 9,)), dma((slots1 + 3,)),
+            pltpu.VMEM((chunk, 2 * lines * width), jnp.float32),
         ],
         compiler_params=pltpu.CompilerParams(
             collective_id=0, has_side_effects=True, vmem_limit_bytes=67043328

time: 393 us -> 385 us (0.980)
  Pallas kernels: 385 us -> 376 us
    pallas_call x1, Pallas kernels: 385 us -> 376 us  [routed(): pl.pallas_call(functools.partial(kernel, sizes), out_shape=jax.ShapeDtype...]
where the time goes in v2:
time: 385 us; the launch traced here: 383 us
  Pallas kernels  376 us (98%)
  local copies, waits for them, and re-layouts  7.32 us (2%)
    pallas_call x1, Pallas kernels, routed(): pl.pallas_call(functools.partial(kernel, sizes), out_shape=jax.ShapeDtype...  376 us

profile of v2, /device:TPU:0, one launch (start us, length us, event | category | flops | bytes accessed | tf_op | source)
XLA Modules:
  0.0 383.2 jit_solution(1076407022548438813)
XLA Ops:
  0.0 375.9 %shard_map.28 = bf16[4,2048,512]{2,1,0:T(8,128)(2,1)} custom-call(bf16[8,2048,256]{2,1,0:T(8,128)(2,1)} %x_ref.1, bf16[8,512,1024]{2,1,0:T(8,128)(2,1)} %y_ref.1), custom_call_target="tpu_custom_call" | custom-call | tf_op jit(solution)/shard_map/pallas_call | solution.py:539
  375.9 7.3 %copy.4 = bf16[4,2048,512]{2,1,0:T(8,128)(2,1)} copy(bf16[4,2048,512]{2,1,0:T(8,128)(2,1)} %shard_map.28) | data formatting | bytes 16777216

commit v3 on v2

--- a/solution.py
+++ b/solution.py
@@ -24,6 +24,9 @@
     return summed.astype(jnp.bfloat16)
 
 
+HALVES = 2
+
+
 def plan():
     recv = {}
 
@@ -33,8 +36,9 @@
     for rel in range(4):
         for ec in range(2):
             for ex in range(2):
-                if rel or ec or ex:
-                    add("x0", rel, ec, ex)
+                for h in range(HALVES):
+                    if rel or ec or ex:
+                        add("x0", rel, ec, ex, h)
     for ec in range(2):
         for ex in range(2):
             if ec or ex:
@@ -50,7 +54,7 @@
 
 
 RECV = plan()
-SENDS = 48
+SENDS = 80
 
 
 def kernel(
@@ -69,7 +73,7 @@
     count = height // chunk
     slots0, slots1 = og0.shape[0], og1.shape[0]
     last, wide = count - 1, lines * width
-    tails = [(0, chunk // 2), (chunk // 2, chunk // 4), (3 * chunk // 4, chunk // 4)]
+    tails = [(j * chunk // 4, chunk // 4) for j in range(4)]
 
     half = z // 2
     mid, end = 1 + half, 3 * half
@@ -109,6 +113,9 @@
         at = lax.rem(level[rel], 2) * lines * width + line(ex) * width
         return yg1.at[pl.ds(pl.multiple_of(at, width), width), ycols(ec, er)]
 
+    def half_rows(h):
+        return pl.ds(h * (height // HALVES), height // HALVES)
+
     def rowsof(r):
         return pl.ds(pl.multiple_of(r * chunk, chunk), chunk)
 
@@ -139,8 +146,8 @@
         cp.start()
         log.append(cp)
 
-    def await_x0(rel, ec, ex):
-        landed(xg.at[0, :, xcols(rel, ec, ex)], recv_sem.at[RECV["x0", rel, ec, ex]])
+    def await_x0(rel, ec, ex, h):
+        landed(xg.at[0, half_rows(h), xcols(rel, ec, ex)], recv_sem.at[RECV["x0", rel, ec, ex, h]])
 
     def await_x1(ec, ex):
         landed(xg.at[1, :, xcols(0, ec, ex)], recv_sem.at[RECV["x1", ec, ex]])
@@ -151,10 +158,10 @@
     def await_y1(rel, ec, ex, er):
         landed(y1zone(rel, ec, ex, er), recv_sem.at[RECV["y1", rel, ec, ex, er]])
 
-    def send_x0(log, rel, ec, ex, to, there):
-        zone = xg.at[0, :, xcols(rel, ec, ex)]
-        src = zone if rel or ec or ex else x_ref.at[batch(0, 0, 0)]
-        push(log, src, zone, ("x0", there, ec, ex), to)
+    def send_x0(log, rel, ec, ex, h, to, there):
+        zone = xg.at[0, half_rows(h), xcols(rel, ec, ex)]
+        src = zone if rel or ec or ex else x_ref.at[batch(0, 0, 0), half_rows(h)]
+        push(log, src, zone, ("x0", there, ec, ex, h), to)
 
     def send_y0(log, ec, ex):
         zone = y0zone(ec, ex, 0)
@@ -166,31 +173,26 @@
         src = zone if rel or ec or ex else y_ref.at[batch(0, 0, 1)]
         push(log, src, zone, ("y1", there, ec, ex, er), to)
 
-    def spread(ec, ex):
+    def spread(ec, ex, what, h=0):
         to = dev(y, z, line(ex), core(ec))
-        own = (0, 0)
-        push(sent, x_ref.at[batch(ec, ex, 0)], xg.at[0, :, xcols(0, *own)], ("x0", 0, ec, ex), to)
-        push(sent, y_ref.at[batch(ec, ex, 1)], y1zone(0, *own, 0), ("y1", 0, ec, ex, 0), to)
-        push(sent, x_ref.at[batch(ec, ex, 1)], xg.at[1, :, xcols(0, *own)], ("x1", ec, ex), to)
-        push(sent, y_ref.at[batch(ec, ex, 0)], y0zone(*own, 0), ("y0", ec, ex, 0), to)
-
-    def spread_line():
-        own = (0, 0)
-        for what in range(4):
-            for ec in range(2):
-                to = dev(y, z, line(1), core(ec))
-                if what == 0:
-                    push(sent, x_ref.at[batch(ec, 1, 0)], xg.at[0, :, xcols(0, *own)], ("x0", 0, ec, 1), to)
-                elif what == 1:
-                    push(sent, y_ref.at[batch(ec, 1, 1)], y1zone(0, *own, 0), ("y1", 0, ec, 1, 0), to)
-                elif what == 2:
-                    push(sent, x_ref.at[batch(ec, 1, 1)], xg.at[1, :, xcols(0, *own)], ("x1", ec, 1), to)
-                else:
-                    push(sent, y_ref.at[batch(ec, 1, 0)], y0zone(*own, 0), ("y0", ec, 1, 0), to)
-
-    send_x0(sent, 0, 0, 0, over_half, 1)
-    spread(1, 0)
-    spread_line()
+        if what == "x0":
+            push(sent, x_ref.at[batch(ec, ex, 0), half_rows(h)], xg.at[0, half_rows(h), xcols(0, 0, 0)],
+                 ("x0", 0, ec, ex, h), to)
+        elif what == "y1":
+            push(sent, y_ref.at[batch(ec, ex, 1)], y1zone(0, 0, 0, 0), ("y1", 0, ec, ex, 0), to)
+        elif what == "x1":
+            push(sent, x_ref.at[batch(ec, ex, 1)], xg.at[1, :, xcols(0, 0, 0)], ("x1", ec, ex), to)
+        else:
+            push(sent, y_ref.at[batch(ec, ex, 0)], y0zone(0, 0, 0), ("y0", ec, ex, 0), to)
+
+    send_x0(sent, 0, 0, 0, 0, over_half, 1)
+    for targets in (((1, 0),), ((0, 1), (1, 1))):
+        for h in range(HALVES):
+            for ec, ex in targets:
+                spread(ec, ex, "x0", h)
+        for what in ("y1", "x1", "y0"):
+            for ec, ex in targets:
+                spread(ec, ex, what)
     keeps = [
         pltpu.make_async_copy(x_ref.at[batch(0, 0, s)], xg.at[s, :, xcols(0, 0, 0)], local_sem.at[s]) for s in range(2)
     ] + [
@@ -339,21 +341,24 @@
     @pl.when(inner)
     def _():
         log = list(sent)
-        send_x0(log, 0, 0, 0, over_mid, 2)
+        send_x0(log, 0, 0, 0, 0, over_mid, 2)
         send_y1(log, 0, 0, 0, over_y, 0, 1)
 
-        def own(ec, ex):
-            await_x0(0, ec, ex)
-            send_x0(log, 0, ec, ex, over_mid, 2)
-            send_x0(log, 0, ec, ex, over_half, 1)
-
-        def outer(ec, ex):
-            await_x0(1, ec, ex)
-            send_x0(log, 1, ec, ex, over_mid, 3)
-
-        def other(rel, ec, ex):
-            await_x0(rel, ec, ex)
-            send_x0(log, rel, ec, ex, over_half, rel)
+        def own_mid(ec, ex, h):
+            if ec or ex:
+                await_x0(0, ec, ex, h)
+            send_x0(log, 0, ec, ex, h, over_mid, 2)
+
+        def own_half(ec, ex, h):
+            send_x0(log, 0, ec, ex, h, over_half, 1)
+
+        def outer(ec, ex, h):
+            await_x0(1, ec, ex, h)
+            send_x0(log, 1, ec, ex, h, over_mid, 3)
+
+        def other(rel, ec, ex, h):
+            await_x0(rel, ec, ex, h)
+            send_x0(log, rel, ec, ex, h, over_half, rel)
 
         def side0(ec, ex):
             await_y0(ec, ex, 0)
@@ -363,37 +368,51 @@
             await_y1(rel, ec, ex, 0)
             send_y1(log, rel, ec, ex, over_y, rel, 1)
 
-        own(1, 0)
+        own_mid(1, 0, 0)
+        own_half(1, 0, 0)
         side1(0, 1, 0)
         send_y0(log, 0, 0)
-        own(0, 1)
-        outer(0, 0)
-        other(2, 0, 0)
-        own(1, 1)
-        outer(1, 0)
-        other(2, 1, 0)
+        side0(1, 0)
+        for ex_ec in ((0, 1), (1, 1)):
+            own_mid(*ex_ec, 0)
+            own_half(*ex_ec, 0)
+        every = ((0, 0), (1, 0), (0, 1), (1, 1))
+        for at in every:
+            outer(*at, 0)
+            other(2, *at, 0)
+        for at in every:
+            own_mid(*at, 1)
+        other(3, 0, 0, 0)
+        outer(0, 0, 1)
+        other(3, 1, 0, 0)
+        outer(1, 0, 1)
         side1(0, 0, 1)
-        other(2, 0, 1)
+        other(3, 0, 1, 0)
+        outer(0, 1, 1)
+        other(3, 1, 1, 0)
+        outer(1, 1, 1)
+        for at in every:
+            own_half(*at, 1)
+        side1(0, 1, 1)
+        other(2, 0, 0, 1)
         side1(1, 0, 0)
-        side1(0, 1, 1)
+        other(2, 1, 0, 1)
+        other(2, 0, 1, 1)
+        other(2, 1, 1, 1)
         side1(1, 1, 0)
-        side0(1, 0)
-        other(2, 1, 1)
-        outer(0, 1)
-        other(3, 0, 0)
-        outer(1, 1)
-        other(3, 1, 0)
         keeps[1].wait()
         await_x1(1, 0)
         await_x1(0, 1)
         await_x1(1, 1)
         send_near(0)
         send_near(1)
+        other(3, 0, 0, 1)
+        other(3, 1, 0, 1)
         side1(1, 0, 1)
-        other(3, 0, 1)
+        other(3, 0, 1, 1)
         side0(0, 1)
+        other(3, 1, 1, 1)
         side1(1, 1, 1)
-        other(3, 1, 1)
         side0(1, 1)
         for r in range(ahead):
             send_far(r)
@@ -425,16 +444,16 @@
             def _():
                 send_tails()
 
-            @pl.when(r == 3)
+            @pl.when(r == 2)
             def _():
                 for ec in range(2):
                     for ex in range(2):
                         await_y0(ec, ex, 1)
 
-            @pl.when((r >= 3) & (r < 7))
+            @pl.when((r >= 2) & (r < 6))
             def _():
                 def step(k, _):
-                    product0((r - 3) * (count // 4) + k)
+                    product0((r - 2) * (count // 4) + k)
                     return 0
 
                 lax.fori_loop(0, count // 4, step, 0)
@@ -467,9 +486,10 @@
     def _():
         log = list(sent)
 
-        def own(ec, ex):
-            await_x0(0, ec, ex)
-            send_x0(log, 0, ec, ex, over_half, 1)
+        def own(ec, ex, h):
+            if ec or ex:
+                await_x0(0, ec, ex, h)
+            send_x0(log, 0, ec, ex, h, over_half, 1)
 
         def side0(ec, ex):
             await_y0(ec, ex, 0)
@@ -480,15 +500,15 @@
                 await_y1(0, ec, ex, 0)
             send_y1(log, 0, ec, ex, over_half, 1, 0)
 
-        own(1, 0)
-        down(0, 0)
-        down(1, 0)
+        own(1, 0, 0)
         send_y0(log, 0, 0)
         side0(1, 0)
-        own(0, 1)
-        own(1, 1)
-        down(0, 1)
-        down(1, 1)
+        own(0, 1, 0)
+        own(1, 1, 0)
+        for at in ((0, 0), (1, 0), (0, 1), (1, 1)):
+            own(*at, 1)
+        for at in ((0, 0), (1, 0), (0, 1), (1, 1)):
+            down(*at)
         keeps[1].wait()
         await_x1(1, 0)
         await_x1(0, 1)
@@ -504,12 +524,17 @@
         for ec in range(2):
             for ex in range(2):
                 await_y0(ec, ex, 1)
-        for rel in range(1, 4):
-            for ec in range(2):
-                for ex in range(2):
-                    await_x0(rel, ec, ex)
-
         def step(k, _):
+            @pl.when(lax.rem(k, count // HALVES) == 0)
+            def _():
+                for h in range(HALVES):
+                    @pl.when(k == h * (count // HALVES))
+                    def _():
+                        for rel in range(1, 4):
+                            for ec in range(2):
+                                for ex in range(2):
+                                    await_x0(rel, ec, ex, h)
+
             product0(k)
             return 0
 
@@ -548,8 +573,8 @@
             pltpu.VMEM((slots0, chunk, lines * width), jnp.bfloat16),
             pltpu.VMEM((slots1, chunk, 2 * lines * width), jnp.bfloat16),
             dma((4,)), dma((SENDS,)), dma((len(RECV),)),
-            dma((2 * count,)), dma((2 * count,)), dma((2 * count,)), dma((2 * count + 4,)), dma((2 * count,)), dma((2 * count + 4,)),
-            dma((slots0,)), dma((slots0,)), dma((3 * slots1 + 9,)), dma((slots1 + 3,)),
+            dma((2 * count,)), dma((2 * count,)), dma((2 * count,)), dma((2 * count + 6,)), dma((2 * count,)), dma((2 * count + 6,)),
+            dma((slots0,)), dma((slots0,)), dma((3 * slots1 + 12,)), dma((slots1 + 4,)),
             pltpu.VMEM((chunk, 2 * lines * width), jnp.float32),
         ],
         compiler_params=pltpu.CompilerParams(

time: 385 us -> 382 us (level)
  no operation moved by 1% of the time
where the time goes in v3:
time: 382 us
  Pallas kernels  375 us (98%)
  local copies, waits for them, and re-layouts  7.32 us (2%)
    pallas_call x1, Pallas kernels, routed(): pl.pallas_call(functools.partial(kernel, sizes), out_shape=jax.ShapeDtype...  375 us

profile of v3, /device:TPU:0, one launch (start us, length us, event | category | flops | bytes accessed | tf_op | source)
XLA Modules:
  0.0 382.2 jit_solution(16545049448141712752)
XLA Ops:
  0.0 374.9 %shard_map.28 = bf16[4,2048,512]{2,1,0:T(8,128)(2,1)} custom-call(bf16[8,2048,256]{2,1,0:T(8,128)(2,1)} %x_ref.1, bf16[8,512,1024]{2,1,0:T(8,128)(2,1)} %y_ref.1), custom_call_target="tpu_custom_call" | custom-call | tf_op jit(solution)/shard_map/pallas_call | solution.py:564
  374.9 7.3 %copy.4 = bf16[4,2048,512]{2,1,0:T(8,128)(2,1)} copy(bf16[4,2048,512]{2,1,0:T(8,128)(2,1)} %shard_map.28) | data formatting | bytes 16777216

commit v4 on v3

--- a/solution.py
+++ b/solution.py
@@ -58,9 +58,8 @@
 
 
 def kernel(
-    sizes, x_ref, y_ref, o_ref, xg, yg0, yg1, og0, og1,
-    local_sem, send_sem, recv_sem, up_send, up_recv, near_send, far_send, near_recv, far_recv,
-    o0_send, o0_keep, o1_send, o1_keep, acc,
+    sizes, x_ref, y_ref, o_ref, x0g, xg, xc, yg0, yg1, og0, og1, acc,
+    local_sem, send_sem, recv_sem, up_send, up_recv, near_send, far_send, near_recv, far_recv, o0_send, o1_send,
 ):
     rows, planes, lines, layers = sizes
     y, col, c = lax.axis_index("row"), lax.axis_index("col"), lax.axis_index("layer")
@@ -147,10 +146,10 @@
         log.append(cp)
 
     def await_x0(rel, ec, ex, h):
-        landed(xg.at[0, half_rows(h), xcols(rel, ec, ex)], recv_sem.at[RECV["x0", rel, ec, ex, h]])
+        landed(x0g.at[half_rows(h), xcols(rel, ec, ex)], recv_sem.at[RECV["x0", rel, ec, ex, h]])
 
     def await_x1(ec, ex):
-        landed(xg.at[1, :, xcols(0, ec, ex)], recv_sem.at[RECV["x1", ec, ex]])
+        landed(xg.at[:, xcols(0, ec, ex)], recv_sem.at[RECV["x1", ec, ex]])
 
     def await_y0(ec, ex, er):
         landed(y0zone(ec, ex, er), recv_sem.at[RECV["y0", ec, ex, er]])
@@ -159,7 +158,7 @@
         landed(y1zone(rel, ec, ex, er), recv_sem.at[RECV["y1", rel, ec, ex, er]])
 
     def send_x0(log, rel, ec, ex, h, to, there):
-        zone = xg.at[0, half_rows(h), xcols(rel, ec, ex)]
+        zone = x0g.at[half_rows(h), xcols(rel, ec, ex)]
         src = zone if rel or ec or ex else x_ref.at[batch(0, 0, 0), half_rows(h)]
         push(log, src, zone, ("x0", there, ec, ex, h), to)
 
@@ -176,12 +175,12 @@
     def spread(ec, ex, what, h=0):
         to = dev(y, z, line(ex), core(ec))
         if what == "x0":
-            push(sent, x_ref.at[batch(ec, ex, 0), half_rows(h)], xg.at[0, half_rows(h), xcols(0, 0, 0)],
+            push(sent, x_ref.at[batch(ec, ex, 0), half_rows(h)], x0g.at[half_rows(h), xcols(0, 0, 0)],
                  ("x0", 0, ec, ex, h), to)
         elif what == "y1":
             push(sent, y_ref.at[batch(ec, ex, 1)], y1zone(0, 0, 0, 0), ("y1", 0, ec, ex, 0), to)
         elif what == "x1":
-            push(sent, x_ref.at[batch(ec, ex, 1)], xg.at[1, :, xcols(0, 0, 0)], ("x1", ec, ex), to)
+            push(sent, x_ref.at[batch(ec, ex, 1)], xg.at[:, xcols(0, 0, 0)], ("x1", ec, ex), to)
         else:
             push(sent, y_ref.at[batch(ec, ex, 0)], y0zone(0, 0, 0), ("y0", ec, ex, 0), to)
 
@@ -193,57 +192,77 @@
         for what in ("y1", "x1", "y0"):
             for ec, ex in targets:
                 spread(ec, ex, what)
+    def staged(i):
+        return xc.at[:, pl.ds(i * depth_x, depth_x)]
+
     keeps = [
-        pltpu.make_async_copy(x_ref.at[batch(0, 0, s)], xg.at[s, :, xcols(0, 0, 0)], local_sem.at[s]) for s in range(2)
-    ] + [
-        pltpu.make_async_copy(y_ref.at[batch(0, 0, 0)], y0zone(0, 0, 0), local_sem.at[2]),
-        pltpu.make_async_copy(y_ref.at[batch(0, 0, 1)], y1zone(0, 0, 0, 0), local_sem.at[3]),
+        pltpu.make_async_copy(x_ref.at[batch(0, 0, 1)], xg.at[:, xcols(0, 0, 0)], local_sem.at[0]),
+        pltpu.make_async_copy(y_ref.at[batch(0, 0, 0)], y0zone(0, 0, 0), local_sem.at[1]),
+        pltpu.make_async_copy(y_ref.at[batch(0, 0, 1)], y1zone(0, 0, 0, 0), local_sem.at[2]),
     ]
-    for keep in keeps:
+    loads = [
+        pltpu.make_async_copy(x_ref.at[batch(0, 0, 0), rowsof(i)], staged(i), local_sem.at[4 + i]) for i in range(count)
+    ]
+    stores = [
+        pltpu.make_async_copy(staged(i), x0g.at[rowsof(i), xcols(0, 0, 0)], local_sem.at[4 + count + i])
+        for i in range(count)
+    ]
+    for keep in loads + keeps:
         keep.start()
 
-    def out0(k, e):
+    def place_own():
+        for load, store in zip(loads, stores):
+            load.wait()
+            store.start()
+
+    def placed_own():
+        for store in stores:
+            store.wait()
+
+    def dot(a, b):
+        return lax.dot_general(a, b, NT, preferred_element_type=jnp.float32).astype(jnp.bfloat16)
+
+    def out0(k):
         slot = lax.rem(k, slots0)
-        src = og0.at[slot, :, tile(line(e))]
-        dst = o_ref.at[x * 2, rowsof(k)]
-        if e == 0:
-            return pltpu.make_async_copy(src, dst, o0_keep.at[slot])
-        return remote(src, dst, o0_send.at[slot], recv_sem.at[RECV[("out0",)]], dev(y, z, line(1), c))
-
-    def free0(k):
-        out0(k, 0).wait()
-        out0(k, 1).wait_send()
+        return remote(og0.at[slot], o_ref.at[x * 2, rowsof(k)], o0_send.at[slot], recv_sem.at[RECV[("out0",)]],
+                      dev(y, z, line(1), c))
 
     def product0(k):
-        pl.when(k >= slots0)(lambda: free0(k - slots0))
-        og0[lax.rem(k, slots0)] = lax.dot_general(
-            xg[0, rowsof(k), :], yg0[...], NT, preferred_element_type=jnp.float32
-        ).astype(jnp.bfloat16)
-        out0(k, 0).start()
-        out0(k, 1).start()
+        load = pltpu.make_async_copy(x0g.at[rowsof(k)], xc, local_sem.at[3])
+        load.start()
+        pl.when(k >= slots0)(lambda: out0(k - slots0).wait_send())
+        load.wait()
+        og0[lax.rem(k, slots0)] = dot(xc[...], yg0[tile(line(1)), :])
+        out0(k).start()
+        o_ref[x * 2, rowsof(k)] = dot(xc[...], yg0[tile(x), :])
+
+    TARGETS = ((1, 1), (1, 0), (0, 1))
+
+    def out_part(src, dst, sem, ez, ex):
+        kind = "out1" if ez == 0 or ex == 0 else "out2"
+        return remote(src, dst, sem, recv_sem.at[RECV[(kind,)]], dev(y, level[ez], line(ex), c))
+
+    def place(ez, ex):
+        return tile(line(ex) if ez else lines)
 
     def out1(r, ez, ex):
         slot = lax.rem(r, slots1)
-        zz = lax.rem(level[ez], 2)
-        src = og1.at[slot, :, tile(zz * lines + line(ex))]
-        dst = o_ref.at[x * 2 + 1, rowsof(r)]
-        if not ez and not ex:
-            return pltpu.make_async_copy(src, dst, o1_keep.at[slot])
-        kind = "out1" if ez == 0 or ex == 0 else "out2"
-        return remote(src, dst, o1_send.at[slot * 3 + ez * 2 + ex - 1], recv_sem.at[RECV[(kind,)]],
-                      dev(y, level[ez], line(ex), c))
+        return out_part(og1.at[slot, :, place(ez, ex)], o_ref.at[x * 2 + 1, rowsof(r)],
+                        o1_send.at[slot * 3 + ez * 2 + ex - 1], ez, ex)
 
     def free1(r):
-        out1(r, 0, 0).wait()
-        for ez, ex in ((1, 1), (1, 0), (0, 1)):
-            out1(r, ez, ex).wait_send()
+        for at in TARGETS:
+            out1(r, *at).wait_send()
+
+    def whose(ez, ex):
+        return tile(lax.rem(level[ez], 2) * lines + line(ex))
 
     def near(r, ec, to, sems):
-        zone = xg.at[1, rowsof(r), xpair(0, ec)]
+        zone = xg.at[rowsof(r), xpair(0, ec)]
         return remote(zone, zone, near_send.at[r * 2 + ec], sems.at[r * 2 + ec], to)
 
     def far(r, ec):
-        zone = xg.at[1, rowsof(r), xpair(1, ec)]
+        zone = xg.at[rowsof(r), xpair(1, ec)]
         return remote(zone, zone, far_send.at[r * 2 + ec], far_recv.at[r * 2 + ec], over_mid)
 
     def send_near(r):
@@ -252,50 +271,40 @@
 
     def far_tail(j, ec):
         at, size = tails[j]
-        zone = xg.at[1, pl.ds(last * chunk + at, size), xpair(1, ec)]
+        zone = xg.at[pl.ds(last * chunk + at, size), xpair(1, ec)]
         k = (last + j) * 2 + ec
         return remote(zone, zone, far_send.at[k], far_recv.at[k], over_mid)
 
     def send_far(r):
         for ec in range(2):
-            landed(xg.at[1, rowsof(r), xpair(1, ec)], up_recv.at[r * 2 + ec])
+            landed(xg.at[rowsof(r), xpair(1, ec)], up_recv.at[r * 2 + ec])
             far(r, ec).start()
 
     def send_tails():
         for ec in range(2):
-            landed(xg.at[1, rowsof(last), xpair(1, ec)], up_recv.at[last * 2 + ec])
+            landed(xg.at[rowsof(last), xpair(1, ec)], up_recv.at[last * 2 + ec])
         for j in range(len(tails)):
             for ec in range(2):
                 far_tail(j, ec).start()
 
     def product1(r):
         for ec in range(2):
-            landed(xg.at[1, rowsof(r), xpair(2, ec)], near_recv.at[r * 2 + ec])
-            landed(xg.at[1, rowsof(r), xpair(3, ec)], far_recv.at[r * 2 + ec])
+            landed(xg.at[rowsof(r), xpair(2, ec)], near_recv.at[r * 2 + ec])
+            landed(xg.at[rowsof(r), xpair(3, ec)], far_recv.at[r * 2 + ec])
         pl.when(r >= slots1)(lambda: free1(r - slots1))
         slot = lax.rem(r, slots1)
-
-        def part(q, _):
-            at = pl.ds(pl.multiple_of(q * wide, wide), wide)
-            og1[slot, :, at] = lax.dot_general(
-                xg[1, rowsof(r), :], yg1[at, :], NT, preferred_element_type=jnp.float32
-            ).astype(jnp.bfloat16)
-            return 0
-
-        lax.fori_loop(0, 2, part, 0)
-        for ez, ex in ((1, 1), (1, 0), (0, 1), (0, 0)):
-            out1(r, ez, ex).start()
+        og1[slot, :, pl.ds(0, wide)] = dot(xg[rowsof(r), :], yg1[half_cols(lax.rem(partner, 2)), :])
+        out1(r, 1, 1).start()
+        out1(r, 1, 0).start()
+        og1[slot, :, place(0, 1)] = dot(xg[rowsof(r), :], yg1[whose(0, 1), :])
+        out1(r, 0, 1).start()
+        o_ref[x * 2 + 1, rowsof(r)] = dot(xg[rowsof(r), :], yg1[whose(0, 0), :])
 
     def out_tail(j, ez, ex):
         at, size = tails[j]
-        zz = lax.rem(level[ez], 2)
-        src = og1.at[last % slots1, pl.ds(at, size), tile(zz * lines + line(ex))]
-        dst = o_ref.at[x * 2 + 1, pl.ds(last * chunk + at, size)]
-        if not ez and not ex:
-            return pltpu.make_async_copy(src, dst, o1_keep.at[slots1 + j])
-        kind = "out1" if ez == 0 or ex == 0 else "out2"
-        return remote(src, dst, o1_send.at[(slots1 + j) * 3 + ez * 2 + ex - 1], recv_sem.at[RECV[(kind,)]],
-                      dev(y, level[ez], line(ex), c))
+        return out_part(og1.at[last % slots1, pl.ds(at, size), place(ez, ex)],
+                        o_ref.at[x * 2 + 1, pl.ds(last * chunk + at, size)],
+                        o1_send.at[(slots1 + j) * 3 + ez * 2 + ex - 1], ez, ex)
 
     def members(ec, far_part):
         third = planes - 1
@@ -308,7 +317,7 @@
         total = None
         for ec in range(2):
             at = members(ec, far_part)
-            term = lax.dot_general(xg[1, rows_at, at], yg1[cols_at, at], NT, preferred_element_type=jnp.float32)
+            term = lax.dot_general(xg[rows_at, at], yg1[cols_at, at], NT, preferred_element_type=jnp.float32)
             total = term if total is None else total + term
         return total
 
@@ -317,7 +326,7 @@
 
     def product_last():
         for ec in range(2):
-            landed(xg.at[1, rowsof(last), xpair(2, ec)], near_recv.at[last * 2 + ec])
+            landed(xg.at[rowsof(last), xpair(2, ec)], near_recv.at[last * 2 + ec])
 
         def part(q, _):
             acc[:, half_cols(q)] = terms(rowsof(last), half_cols(q), False)
@@ -327,14 +336,18 @@
         free1(last - slots1)
         for j, (at, size) in enumerate(tails):
             for ec in range(2):
-                landed(xg.at[1, pl.ds(last * chunk + at, size), xpair(3, ec)], far_recv.at[(last + j) * 2 + ec])
-            for ez in (1, 0):
-                cols_at = half_cols(lax.rem(level[ez], 2))
-                og1[last % slots1, pl.ds(at, size), cols_at] = (
-                    acc[pl.ds(at, size), cols_at] + terms(pl.ds(last * chunk + at, size), cols_at, True)
-                ).astype(jnp.bfloat16)
-                for ex in (1, 0):
-                    out_tail(j, ez, ex).start()
+                landed(xg.at[pl.ds(last * chunk + at, size), xpair(3, ec)], far_recv.at[(last + j) * 2 + ec])
+
+            def final(cols_at):
+                more = terms(pl.ds(last * chunk + at, size), cols_at, True)
+                return (acc[pl.ds(at, size), cols_at] + more).astype(jnp.bfloat16)
+
+            og1[last % slots1, pl.ds(at, size), pl.ds(0, wide)] = final(half_cols(lax.rem(partner, 2)))
+            out_tail(j, 1, 1).start()
+            out_tail(j, 1, 0).start()
+            og1[last % slots1, pl.ds(at, size), place(0, 1)] = final(whose(0, 1))
+            out_tail(j, 0, 1).start()
+            o_ref[x * 2 + 1, pl.ds(last * chunk + at, size)] = final(whose(0, 0))
 
     ahead = 4
 
@@ -373,6 +386,7 @@
         side1(0, 1, 0)
         send_y0(log, 0, 0)
         side0(1, 0)
+        place_own()
         for ex_ec in ((0, 1), (1, 1)):
             own_mid(*ex_ec, 0)
             own_half(*ex_ec, 0)
@@ -400,7 +414,7 @@
         other(2, 0, 1, 1)
         other(2, 1, 1, 1)
         side1(1, 1, 0)
-        keeps[1].wait()
+        keeps[0].wait()
         await_x1(1, 0)
         await_x1(0, 1)
         await_x1(1, 1)
@@ -417,9 +431,9 @@
         for r in range(ahead):
             send_far(r)
             send_near(r + 2)
-        keeps[0].wait()
+        placed_own()
+        keeps[1].wait()
         keeps[2].wait()
-        keeps[3].wait()
         for rel in range(2):
             for ec in range(2):
                 for ex in range(2):
@@ -470,13 +484,12 @@
         for j in range(len(tails)):
             for ec in range(2):
                 far_tail(j, ec).wait_send()
-            for ez, ex in ((1, 1), (1, 0), (0, 1)):
-                out_tail(j, ez, ex).wait_send()
-            out_tail(j, 0, 0).wait()
+            for at in TARGETS:
+                out_tail(j, *at).wait_send()
         for r in range(count - slots1, last):
             free1(r)
         for k in range(count - slots0, count):
-            free0(k)
+            out0(k).wait_send()
         landed(o_ref.at[line(1) * 2], recv_sem.at[RECV[("out0",)]])
         landed(o_ref.at[line(1) * 2 + 1], recv_sem.at[RECV[("out1",)]])
         for cp in log:
@@ -503,13 +516,14 @@
         own(1, 0, 0)
         send_y0(log, 0, 0)
         side0(1, 0)
+        place_own()
         own(0, 1, 0)
         own(1, 1, 0)
         for at in ((0, 0), (1, 0), (0, 1), (1, 1)):
             own(*at, 1)
         for at in ((0, 0), (1, 0), (0, 1), (1, 1)):
             down(*at)
-        keeps[1].wait()
+        keeps[0].wait()
         await_x1(1, 0)
         await_x1(0, 1)
         await_x1(1, 1)
@@ -518,9 +532,9 @@
                 near(r, ec, over_half, up_recv).start()
         side0(0, 1)
         side0(1, 1)
-        keeps[0].wait()
+        placed_own()
+        keeps[1].wait()
         keeps[2].wait()
-        keeps[3].wait()
         for ec in range(2):
             for ex in range(2):
                 await_y0(ec, ex, 1)
@@ -543,7 +557,7 @@
             for ec in range(2):
                 near(r, ec, over_half, up_recv).wait_send()
         for k in range(count - slots0, count):
-            free0(k)
+            out0(k).wait_send()
         landed(o_ref.at[line(1) * 2], recv_sem.at[RECV[("out0",)]])
         landed(o_ref.at[x * 2 + 1], recv_sem.at[RECV[("out1",)]])
         landed(o_ref.at[line(1) * 2 + 1], recv_sem.at[RECV[("out2",)]])
@@ -556,31 +570,36 @@
     _, height, depth_x = anomaly_x.shape
     width, depth_y = anomaly_y.shape[1:]
     members = depth_y * rows * layers
-    chunk, slots0, slots1 = height // 8, 2, 2
-    count = height // chunk
+    count, slots0, slots1 = 8, 4, 4
+    chunk = height // count
     dma = pltpu.SemaphoreType.DMA
     any_ = pl.BlockSpec(memory_space=pl.ANY)
     kind = anomaly_x.dtype
+    many = dma((2 * count,))
     return pl.pallas_call(
         functools.partial(kernel, sizes),
-        out_shape=jax.ShapeDtypeStruct((planes, height, width), jnp.bfloat16),
+        out_shape=[
+            pltpu.VMEM((planes, height, width), jnp.bfloat16),
+            jax.ShapeDtypeStruct((height, members), kind),
+        ],
         in_specs=[any_, any_],
-        out_specs=any_,
+        out_specs=[pl.BlockSpec(memory_space=pltpu.VMEM), any_],
         scratch_shapes=[
-            pltpu.VMEM((2, height, members), kind),
+            pltpu.VMEM((height, members), kind),
+            pltpu.VMEM((chunk, members), kind),
             pltpu.VMEM((lines * width, members), kind),
             pltpu.VMEM((2 * lines * width, members), kind),
-            pltpu.VMEM((slots0, chunk, lines * width), jnp.bfloat16),
-            pltpu.VMEM((slots1, chunk, 2 * lines * width), jnp.bfloat16),
-            dma((4,)), dma((SENDS,)), dma((len(RECV),)),
-            dma((2 * count,)), dma((2 * count,)), dma((2 * count,)), dma((2 * count + 6,)), dma((2 * count,)), dma((2 * count + 6,)),
-            dma((slots0,)), dma((slots0,)), dma((3 * slots1 + 12,)), dma((slots1 + 4,)),
+            pltpu.VMEM((slots0, chunk, width), jnp.bfloat16),
+            pltpu.VMEM((slots1, chunk, (lines + 1) * width), jnp.bfloat16),
             pltpu.VMEM((chunk, 2 * lines * width), jnp.float32),
+            dma((4 + 2 * count,)), dma((SENDS,)), dma((len(RECV),)),
+            many, many, many, dma((2 * count + 6,)), many, dma((2 * count + 6,)),
+            dma((slots0,)), dma((3 * slots1 + 12,)),
         ],
         compiler_params=pltpu.CompilerParams(
-            collective_id=0, has_side_effects=True, vmem_limit_bytes=67043328
+            collective_id=0, has_side_effects=True, vmem_limit_bytes=54 * 2**20
         ),
-    )(anomaly_x, anomaly_y)
+    )(anomaly_x, anomaly_y)[0]
 
 
 def on_device(mesh, anomaly_x, anomaly_y):

time: 382 us -> 379 us (level)
  local copies, waits for them, and re-layouts: 7.32 us -> 3.4 us
    unnamed x1, local copies, waits for them, and re-layouts: 7.32 us -> 3.4 us
where the time goes in v4:
time: 379 us; the launch traced here: 378 us
  Pallas kernels  375 us (99%)
    pallas_call x1, Pallas kernels, routed(): pl.pallas_call(functools.partial(kernel, sizes), out_shape=[pltpu.VMEM((p...  375 us

profile of v4, /device:TPU:0, one launch (start us, length us, event | category | flops | bytes accessed | tf_op | source)
XLA Modules:
  0.0 378.3 jit_solution(12403986650897822639)
XLA Ops:
  0.0 374.9 %shard_map.28 = (bf16[4,2048,512]{2,1,0:T(8,128)(2,1)S(1)}, bf16[2048,4096]{1,0:T(8,128)(2,1)}) custom-call(bf16[8,2048,256]{2,1,0:T(8,128)(2,1)} %x_ref.1, bf16[8,512,1024]{2,1,0:T(8,128)(2,1)} %y_ref.1), custom_call_target="tpu_custom_call" | custom-call | tf_op jit(solution)/shard_map/pallas_call | solution.py:579
  374.9 3.4 copy.4

commit v5 on v4

--- a/solution.py
+++ b/solution.py
@@ -342,9 +342,9 @@
                 more = terms(pl.ds(last * chunk + at, size), cols_at, True)
                 return (acc[pl.ds(at, size), cols_at] + more).astype(jnp.bfloat16)
 
-            og1[last % slots1, pl.ds(at, size), pl.ds(0, wide)] = final(half_cols(lax.rem(partner, 2)))
-            out_tail(j, 1, 1).start()
-            out_tail(j, 1, 0).start()
+            for ex in (1, 0):
+                og1[last % slots1, pl.ds(at, size), place(1, ex)] = final(whose(1, ex))
+                out_tail(j, 1, ex).start()
             og1[last % slots1, pl.ds(at, size), place(0, 1)] = final(whose(0, 1))
             out_tail(j, 0, 1).start()
             o_ref[x * 2 + 1, pl.ds(last * chunk + at, size)] = final(whose(0, 0))
@@ -475,6 +475,8 @@
             return 0
 
         lax.fori_loop(0, last, both, 0)
+        for cp in log:
+            cp.wait_send()
         product_last()
         for r in range(count):
             for ec in range(2):
@@ -492,8 +494,6 @@
             out0(k).wait_send()
         landed(o_ref.at[line(1) * 2], recv_sem.at[RECV[("out0",)]])
         landed(o_ref.at[line(1) * 2 + 1], recv_sem.at[RECV[("out1",)]])
-        for cp in log:
-            cp.wait_send()
 
     @pl.when(jnp.logical_not(inner))
     def _():
@@ -558,11 +558,11 @@
                 near(r, ec, over_half, up_recv).wait_send()
         for k in range(count - slots0, count):
             out0(k).wait_send()
+        for cp in log:
+            cp.wait_send()
         landed(o_ref.at[line(1) * 2], recv_sem.at[RECV[("out0",)]])
         landed(o_ref.at[x * 2 + 1], recv_sem.at[RECV[("out1",)]])
         landed(o_ref.at[line(1) * 2 + 1], recv_sem.at[RECV[("out2",)]])
-        for cp in log:
-            cp.wait_send()
 
 
 def routed(sizes, anomaly_x, anomaly_y):

time: 379 us -> 378 us (level)
  no operation moved by 1% of the time
where the time goes in v5:
time: 378 us
  Pallas kernels  375 us (99%)
    pallas_call x1, Pallas kernels, routed(): pl.pallas_call(functools.partial(kernel, sizes), out_shape=[pltpu.VMEM((p...  375 us

profile of v5, /device:TPU:0, one launch (start us, length us, event | category | flops | bytes accessed | tf_op | source)
XLA Modules:
  0.0 377.9 jit_solution(5338035049478905757)
XLA Ops:
  0.0 374.5 %shard_map.28 = (bf16[4,2048,512]{2,1,0:T(8,128)(2,1)S(1)}, bf16[2048,4096]{1,0:T(8,128)(2,1)}) custom-call(bf16[8,2048,256]{2,1,0:T(8,128)(2,1)} %x_ref.1, bf16[8,512,1024]{2,1,0:T(8,128)(2,1)} %y_ref.1), custom_call_target="tpu_custom_call" | custom-call | tf_op jit(solution)/shard_map/pallas_call | solution.py:579
  374.5 3.4 copy.4
